TPU v7x, 32 devices: a whole 2x2x4 slice. The times are simulated.
32 devices in a mesh: ep: 4 (over x, core), fsdp: 8 (over z, y).
Axes of the slice: x: 2, y: 2, z: 4, core: 2. Of those that a mesh axis runs over, the one named last changes fastest.
Arguments:
- train_gate: float32 [128, 2048, 768], P('ep', 'fsdp'), may hold values from -0.1875 to 0.1875
- other_gate: bfloat16 [128, 2048, 768], P('ep', 'fsdp'), may hold values from -0.0625 to 0.0625
- train_up: float32 [128, 2048, 768], P('ep', 'fsdp'), may hold values from -0.1875 to 0.1875
- other_up: bfloat16 [128, 2048, 768], P('ep', 'fsdp'), may hold values from -0.0625 to 0.0625
- router_weight: float32 [2048, 128], P('fsdp', 'ep'), may hold values from -0.125 to 0.125
- router_gain: float32 [2048], P('fsdp'), may hold values from 0.25 to 1.75
Outputs:
- ready_gate: bfloat16 [128, 2048, 768], P('ep', None, 'fsdp')
- ready_up: bfloat16 [128, 2048, 768], P('ep', None, 'fsdp')
- scale_gate: float32 [128, 768], P('ep', 'fsdp')
- scale_up: float32 [128, 768], P('ep', 'fsdp')
- serve_router: bfloat16 [2048, 128], replicated
All inputs are finite; a program needn't handle non-finite values. Where the computation divides by a largest or mean magnitude, that divisor is 1e-20 or more.
Results may differ from a plain program's by a relative error of at most 0.001.
Values may be sent and summed in bfloat16 or wider, within the bound.
A program may use at most 256 MiB of HBM per device.

v0:
```python
import functools

import jax
import jax.numpy as jnp
from jax import lax
from jax.experimental import pallas as pl
from jax.experimental.pallas import tpu as pltpu
from jax.sharding import PartitionSpec as P

MESH = pl.DeviceIdType.MESH
SLOTS = 3


def plain_device(train_gate, other_gate, train_up, other_up, router_weight, router_gain):
    latest_gate = train_gate + other_gate.astype(jnp.float32)
    latest_up = train_up + other_up.astype(jnp.float32)
    depth = train_gate.shape[1] * lax.axis_size("fsdp")
    total_gate, total_up = lax.psum(
        (jnp.sum(jnp.abs(latest_gate), axis=1), jnp.sum(jnp.abs(latest_up), axis=1)), "fsdp"
    )
    scale_gate = total_gate / depth
    scale_up = total_up / depth
    narrow_gate = (latest_gate / jnp.expand_dims(scale_gate, 1)).astype(jnp.bfloat16)
    narrow_up = (latest_up / jnp.expand_dims(scale_up, 1)).astype(jnp.bfloat16)
    ready_gate = lax.all_to_all(narrow_gate, "fsdp", split_axis=2, concat_axis=1, tiled=True)
    ready_up = lax.all_to_all(narrow_up, "fsdp", split_axis=2, concat_axis=1, tiled=True)
    width = ready_gate.shape[2]
    start = lax.axis_index("fsdp") * width
    scale_gate = lax.dynamic_slice_in_dim(scale_gate, start, width, axis=1)
    scale_up = lax.dynamic_slice_in_dim(scale_up, start, width, axis=1)
    part_router = (router_weight * router_gain[:, None]).astype(jnp.bfloat16)
    row_router = lax.all_gather(part_router, "fsdp", axis=0, tiled=True)
    serve_router = lax.all_gather(row_router, "ep", axis=1, tiled=True)
    return (ready_gate, ready_up, scale_gate, scale_up, serve_router)


def far_first(n):
    return sorted(range(1, n), key=lambda d: (abs(d - n // 2), d))


def kernel(n, p, tg, og, tu, ou, rw, rgain, ready_gate, ready_up, scale_gate, scale_up, router,
           wide, narrow, send, part_a, land_a, tot_a, part_b, land_b, tot_b, rows_r, all_r,
           in_sem, own_sem, send_sem, recv_sem, small_send, small_recv, r_send, r_recv):
    experts, depth, width = tg.shape
    piece = width // n
    me = lax.axis_index("fsdp")
    group = lax.axis_index("ep")
    first = n // 2
    trains, others = (tg, tu), (og, ou)
    readys, scales = (ready_gate, ready_up), (scale_gate, scale_up)
    peers = [(me + d) % n for d in far_first(n)]
    twins = [(group + d) % p for d in range(1, p)]

    barrier = pltpu.get_barrier_semaphore()
    for peer in peers:
        pl.semaphore_signal(barrier, inc=1, device_id={"fsdp": peer}, device_id_type=MESH)
    for twin in twins:
        pl.semaphore_signal(barrier, inc=1, device_id={"ep": twin}, device_id_type=MESH)

    def loads(e, slot):
        return [
            pltpu.make_async_copy(src.at[e], dst.at[m, slot], in_sem.at[k, m, slot])
            for m in range(2)
            for k, (src, dst) in enumerate(((trains[m], wide), (others[m], narrow)))
        ]

    def over(low, high, body):
        for e in range(low, min(low + SLOTS - 1, high)):
            for copy in loads(e, (e - low) % SLOTS):
                copy.start()

        def step(i, _):
            e = low + i
            slot = lax.rem(i, SLOTS)

            @pl.when(e + SLOTS - 1 < high)
            def _():
                for copy in loads(e + SLOTS - 1, lax.rem(i + SLOTS - 1, SLOTS)):
                    copy.start()

            for copy in loads(e, slot):
                copy.wait()
            for m in range(2):
                body(e, m, slot)
            return 0

        lax.fori_loop(0, high - low, step, 0)

    def sums(base, part, share):
        def body(e, m, slot):
            at = (e - base) * 2 + m
            latest = wide[m, slot] + narrow[m, slot].astype(jnp.float32)
            row = jnp.sum(jnp.abs(latest), axis=0, keepdims=True)
            part[at // share, pl.ds(at % share, 1), :] = row

        return body

    def ready(base, tot, share):
        def body(e, m, slot):
            at = (e - base) * 2 + m
            scale = tot[at // share, pl.ds(at % share, 1), :] / (n * depth)
            scales[m][pl.ds(e, 1), :] = scale
            inverse = 1.0 / scale
            step = 128
            for c in range(0, width, step):
                latest = wide[m, slot, :, c:c + step] + narrow[m, slot, :, c:c + step].astype(jnp.float32)
                value = latest * inverse[:, c:c + step]
                send[m, e, c:c + step, :] = value.T.astype(jnp.bfloat16)
            place = readys[m].at[e, :, pl.ds(pl.multiple_of(me * depth, 128), depth)]
            for peer in peers:
                pltpu.make_async_remote_copy(
                    src_ref=send.at[m, e, pl.ds(pl.multiple_of(peer * piece, 16), piece), :],
                    dst_ref=place,
                    send_sem=send_sem.at[m],
                    recv_sem=recv_sem.at[m],
                    device_id={"fsdp": peer},
                    device_id_type=MESH,
                ).start()
            pltpu.make_async_copy(
                send.at[m, e, pl.ds(pl.multiple_of(me * piece, 16), piece), :], place, own_sem.at[m]
            ).start()

        return body

    def push(src, dst, at, axis, targets, s, r):
        for target, block in zip(targets, src):
            pltpu.make_async_remote_copy(
                src_ref=block, dst_ref=dst.at[at], send_sem=s, recv_sem=r,
                device_id={axis: target}, device_id_type=MESH,
            ).start()

    def drain(ref, sem):
        pltpu.make_async_copy(ref, ref, sem).wait()

    def scatter(part, land, k):
        push([part.at[peer] for peer in peers], land, me, "fsdp", peers, small_send.at[k], small_recv.at[k])
        land[me] = part[me]

    def gather(land, tot, k):
        drain(land.at[pl.ds(0, n - 1)], small_recv.at[k])
        tot[me] = jnp.sum(land[...], axis=0)
        push([tot.at[me]] * (n - 1), tot, me, "fsdp", peers, small_send.at[k + 1], small_recv.at[k + 1])

    def gathered(tot, k):
        drain(tot.at[pl.ds(0, n - 1)], small_recv.at[k + 1])

    share_b = part_b.shape[1]
    over(0, first, sums(0, part_a, 1))
    rows_r[me] = (rw[...] * rgain[...]).astype(jnp.bfloat16)
    pl.semaphore_wait(barrier, n - 1 + p - 1)
    scatter(part_a, land_a, 0)
    gather(land_a, tot_a, 0)
    gathered(tot_a, 0)
    cut = max(first // 2, 1)
    over(0, cut, ready(0, tot_a, 1))
    over(first, experts, sums(first, part_b, share_b))
    scatter(part_b, land_b, 2)
    push([rows_r.at[me]] * (n - 1), rows_r, me, "fsdp", peers, r_send.at[0], r_recv.at[0])
    middle = (cut + first) // 2
    over(cut, middle, ready(0, tot_a, 1))
    gather(land_b, tot_b, 2)
    over(middle, first, ready(0, tot_a, 1))
    gathered(tot_b, 2)
    later = first + (experts - first) // 4
    over(first, later, ready(first, tot_b, share_b))
    drain(rows_r.at[pl.ds(0, n - 1)], r_recv.at[0])
    push([rows_r] * (p - 1), all_r, group, "ep", twins, r_send.at[1], r_recv.at[1])
    all_r[group] = rows_r[...]
    over(later, experts, ready(first, tot_b, share_b))
    if p > 1:
        drain(all_r.at[pl.ds(0, p - 1)], r_recv.at[1])
    for f in range(n):
        block = all_r[:, f].astype(jnp.float32)
        block = block.reshape(block.shape[0] * block.shape[1], depth)
        router[f * depth:(f + 1) * depth, :] = block.T.astype(jnp.bfloat16)
    for k, (part, tot) in enumerate(((part_a, tot_a), (part_b, tot_b))):
        drain(part.at[pl.ds(0, n - 1)], small_send.at[2 * k])
        drain(tot.at[pl.ds(0, n - 1)], small_send.at[2 * k + 1])
    drain(rows_r.at[pl.ds(0, n - 1)], r_send.at[0])
    if p > 1:
        drain(all_r.at[pl.ds(0, p - 1)], r_send.at[1])
    for m in range(2):
        drain(send.at[m, :, pl.ds(0, piece), :], own_sem.at[m])
        drain(send.at[m, :, pl.ds(0, width - piece), :], send_sem.at[m])
        drain(readys[m].at[:, :, pl.ds(0, (n - 1) * depth)], recv_sem.at[m])


def sending_device(n, p, train_gate, other_gate, train_up, other_up, router_weight, router_gain):
    experts, depth, width = train_gate.shape
    piece = width // n
    columns = router_weight.shape[1]
    share = (2 * experts - n) // n
    f32, bf16 = jnp.float32, jnp.bfloat16
    anywhere = pl.BlockSpec(memory_space=pl.ANY)
    vmem = pl.BlockSpec(memory_space=pltpu.VMEM)
    ready = jax.ShapeDtypeStruct((experts, piece, n * depth), bf16)
    scale = jax.ShapeDtypeStruct((experts, width), f32)
    stats = [pltpu.VMEM((n, 1, width), f32)] * 3 + [pltpu.VMEM((n, share, width), f32)] * 3
    dma = pltpu.SemaphoreType.DMA
    ready_gate, ready_up, scale_gate, scale_up, router = pl.pallas_call(
        functools.partial(kernel, n, p),
        out_shape=(ready, ready, scale, scale, jax.ShapeDtypeStruct((n * depth, p * columns), bf16)),
        in_specs=[anywhere] * 4 + [vmem] * 2,
        out_specs=(anywhere, anywhere, vmem, vmem, vmem),
        scratch_shapes=[
            pltpu.VMEM((2, SLOTS, depth, width), f32),
            pltpu.VMEM((2, SLOTS, depth, width), bf16),
            pltpu.VMEM((2, experts, width, depth), bf16),
            *stats,
            pltpu.VMEM((n, columns, depth), bf16),
            pltpu.VMEM((p, n, columns, depth), bf16),
            dma((2, 2, SLOTS)), dma((2,)), dma((2,)), dma((2,)), dma((4,)), dma((4,)), dma((2,)), dma((2,)),
        ],
        compiler_params=pltpu.CompilerParams(
            collective_id=0, has_side_effects=True, vmem_limit_bytes=60 * 2**20
        ),
        name="send_ready",
    )(train_gate, other_gate, train_up, other_up, router_weight.T, router_gain[None, :])
    start = lax.axis_index("fsdp") * piece
    return (
        jnp.swapaxes(ready_gate, 1, 2),
        jnp.swapaxes(ready_up, 1, 2),
        lax.dynamic_slice_in_dim(scale_gate, start, piece, axis=1),
        lax.dynamic_slice_in_dim(scale_up, start, piece, axis=1),
        router,
    )


def solution(mesh):
    n, p = mesh.shape["fsdp"], mesh.shape["ep"]

    def per_device(*args):
        experts, depth, width = args[0].shape
        fits = (
            depth % 128 == 0 and width % (16 * n) == 0 and width % 128 == 0 and n % 2 == 0
            and 2 * experts % n == 0 and 2 * experts > n and args[4].shape[1] % 16 == 0
            and 2 * experts * depth * width * 2 <= 2**25
        )
        return sending_device(n, p, *args) if fits else plain_device(*args)

    matrix = P("ep", "fsdp", None)
    in_specs = (matrix, matrix, matrix, matrix, P("fsdp", "ep"), P("fsdp"))
    out_specs = (P("ep", None, "fsdp"), P("ep", None, "fsdp"), P("ep", "fsdp"), P("ep", "fsdp"), P())
    return jax.shard_map(
        per_device, mesh=mesh, in_specs=in_specs, out_specs=out_specs, check_vma=False
    )
```

profile of v0, /device:TPU:0, one launch (start us, length us, event | category | flops | bytes accessed | tf_op | source)
XLA Modules:
  0.0 590.4 jit_solution(3386432509079304458)
XLA Ops:
  0.6 569.8 %send_ready.1 = (bf16[32,96,2048]{2,1,0:T(8,128)(2,1)}, bf16[32,96,2048]{2,1,0:T(8,128)(2,1)}, f32[32,768]{1,0:T(8,128)}, f32[32,768]{1,0:T(8,128)}, bf16[2048,128]{1,0:T(8,128)(2,1)}) custom-call(f32[32,256,768]{2,1,0:T(8,128)} %tg.1, bf16[32,256,768]{2,1,0:T(8,128)(2,1)} %og.1, f32[32,256,768]{2,1,0:T(8,128)} %tu.1, bf16[32,256,768]{2,1,0:T(8,128)(2,1)} %ou.1, ...), custom_call_target="tpu_custom_call" | custom-call | tf_op jit(solution)/shard_map/send_ready/pallas_call | solution.py:200
  570.5 1.5 constant_dynamic-slice_fusion
  572.0 0.0 copy-start
  572.0 11.4 %copy.14 = bf16[32,2048,96]{1,2,0:T(8,128)(2,1)} copy(bf16[32,2048,96]{1,2,0:T(8,128)(2,1)} %bitcast.5) | data formatting | bytes 25165824
  583.3 1.5 copy-done
  584.9 0.0 copy-start.1
  584.9 4.8 copy.15
  589.6 0.0 copy-done.1
  589.6 0.8 copy.16
Async XLA Ops:
  572.0 12.9 %copy-start = (bf16[32,96,2048]{2,1,0:T(8,128)(2,1)S(1)}, bf16[32,96,2048]{2,1,0:T(8,128)(2,1)}, u32[]{:S(2)}) copy-start(bf16[32,96,2048]{2,1,0:T(8,128)(2,1)} %get-tuple-element.11) | copy-start | bytes 37748740
  584.9 4.8 copy-start.1
where the time goes:
time: 591 us; the launch traced here: 590 us
  Pallas kernels  570 us (96%)
  local copies, waits for them, and re-layouts  20 us (3%)
    pallas_call x1, Pallas kernels, sending_device(): pl.pallas_call(functools.partial(kernel, n, p), out_shape=(ready, ready,...  570 us
    unnamed x7, local copies, waits for them, and re-layouts  18.5 us

commit v1 on v0

v1 whole, which is shorter than its diff:
```python
import functools

import jax
import jax.numpy as jnp
from jax import lax
from jax.experimental import pallas as pl
from jax.experimental.pallas import tpu as pltpu
from jax.sharding import PartitionSpec as P

MESH = pl.DeviceIdType.MESH
SLOTS = 3
RING = 8
LAG = 4
f32, bf16 = jnp.float32, jnp.bfloat16


def plain_device(train_gate, other_gate, train_up, other_up, router_weight, router_gain):
    latest_gate = train_gate + other_gate.astype(jnp.float32)
    latest_up = train_up + other_up.astype(jnp.float32)
    depth = train_gate.shape[1] * lax.axis_size("fsdp")
    total_gate, total_up = lax.psum(
        (jnp.sum(jnp.abs(latest_gate), axis=1), jnp.sum(jnp.abs(latest_up), axis=1)), "fsdp"
    )
    scale_gate = total_gate / depth
    scale_up = total_up / depth
    narrow_gate = (latest_gate / jnp.expand_dims(scale_gate, 1)).astype(jnp.bfloat16)
    narrow_up = (latest_up / jnp.expand_dims(scale_up, 1)).astype(jnp.bfloat16)
    ready_gate = lax.all_to_all(narrow_gate, "fsdp", split_axis=2, concat_axis=1, tiled=True)
    ready_up = lax.all_to_all(narrow_up, "fsdp", split_axis=2, concat_axis=1, tiled=True)
    width = ready_gate.shape[2]
    start = lax.axis_index("fsdp") * width
    scale_gate = lax.dynamic_slice_in_dim(scale_gate, start, width, axis=1)
    scale_up = lax.dynamic_slice_in_dim(scale_up, start, width, axis=1)
    part_router = (router_weight * router_gain[:, None]).astype(jnp.bfloat16)
    row_router = lax.all_gather(part_router, "fsdp", axis=0, tiled=True)
    serve_router = lax.all_gather(row_router, "ep", axis=1, tiled=True)
    return (ready_gate, ready_up, scale_gate, scale_up, serve_router)


def far_first(n):
    return sorted(range(1, n), key=lambda d: (abs(d - n // 2), d))


def drain(ref, sem):
    pltpu.make_async_copy(ref, ref, sem).wait()


class Stream:
    def __init__(self, sources, wide, narrow, sem):
        self.sources, self.wide, self.narrow, self.sem = sources, wide, narrow, sem

    def loads(self, e):
        slot = lax.rem(e, SLOTS)
        return [
            pltpu.make_async_copy(src.at[e], dst.at[m, slot], self.sem.at[k, m, slot])
            for m, pair in enumerate(self.sources)
            for k, (src, dst) in enumerate(zip(pair, (self.wide, self.narrow)))
        ]

    def prime(self, low, last):
        for i in range(SLOTS - 1):
            @pl.when(low + i < last)
            def _():
                for copy in self.loads(low + i):
                    copy.start()

    def one(self, e, last, body):
        @pl.when(e + SLOTS - 1 < last)
        def _():
            for copy in self.loads(e + SLOTS - 1):
                copy.start()

        copies = self.loads(e)
        slot = lax.rem(e, SLOTS)
        for m in range(2):
            copies[2 * m].wait()
            copies[2 * m + 1].wait()
            body(e, m, self.wide.at[m, slot], self.narrow.at[m, slot])

    def run(self, low, high, last, body):
        def step(i, _):
            self.one(low + i, last, body)
            return 0

        lax.fori_loop(0, high - low, step, 0)


def row_sums(wide, narrow, out, at):
    depth, width = wide.shape
    block = 256 if width % 256 == 0 else 128
    for c in range(0, width, block):
        total = jnp.zeros((16, block), f32)
        for r in range(0, depth, 16):
            total += jnp.abs(wide[r:r + 16, c:c + block] + narrow[r:r + 16, c:c + block].astype(f32))
        out[at, c:c + block] = jnp.sum(total, axis=0, keepdims=True)


def sender(n, me, peers, send, scales, readys, base, own_sem, send_sem, recv_sem):
    def body(e, m, wide, narrow):
        depth, width = wide.shape
        piece = width // n
        inverse = 1.0 / scales[m][pl.ds(e, 1), :]
        at = e - base
        for c in range(0, width, 128):
            latest = wide[:, c:c + 128] + narrow[:, c:c + 128].astype(f32)
            value = latest * inverse[:, c:c + 128]
            send[m, at, c:c + 128, :] = value.T.astype(bf16)
        place = readys[m].at[at, :, pl.ds(pl.multiple_of(me * depth, 128), depth)]
        for peer in peers:
            pltpu.make_async_remote_copy(
                src_ref=send.at[m, at, pl.ds(pl.multiple_of(peer * piece, 16), piece), :],
                dst_ref=place,
                send_sem=send_sem.at[m],
                recv_sem=recv_sem.at[m],
                device_id={"fsdp": peer},
                device_id_type=MESH,
            ).start()
        own = send.at[m, at, pl.ds(pl.multiple_of(me * piece, 16), piece), :]
        if own_sem is None:
            place[...] = own[...]
        else:
            pltpu.make_async_copy(own, place, own_sem.at[m]).start()

    return body


def finish(n, count, send, readys, own_sem, send_sem, recv_sem):
    width, depth = send.shape[2:]
    piece = width // n
    for m in range(2):
        some = pl.ds(0, count)
        if own_sem is not None:
            drain(send.at[m, some, pl.ds(0, piece), :], own_sem.at[m])
        drain(send.at[m, some, pl.ds(0, width - piece), :], send_sem.at[m])
        drain(readys[m].at[some, :, pl.ds(0, (n - 1) * depth)], recv_sem.at[m])


def bulk_kernel(n, p, cut, more, tg, og, tu, ou, rw, rgain, ready_gate, ready_up, scale_gate, scale_up, router,
                wide_s, narrow_s, wide_r, narrow_r, send, land_0, part_a, land_a, tot_a,
                part_z, land_z, sum_z, far_z, tot_z, rows_r, all_r,
                in_s, in_r, own_sem, send_sem, recv_sem, small_send, small_recv, r_send, r_recv):
    experts, depth, width = tg.shape
    half = n // 2
    me = lax.axis_index("fsdp")
    group = lax.axis_index("ep")
    odd = lax.rem(group, 2) == 1
    stop = jnp.where(odd, cut + more, cut)
    mine = lax.rem(me, half)
    side = me - mine
    first, second = 1, 1 + half
    readys, scales = (ready_gate, ready_up), (scale_gate, scale_up)
    peers = [(me + d) % n for d in far_first(n)]
    near = [side + lax.rem(mine + d, half) for d in range(1, half)]
    near_at = [lax.rem(mine + d, half) for d in range(1, half)]
    far = (me + half) % n
    twins = [(group + d) % p for d in range(1, p)]
    sources = ((tg, og), (tu, ou))
    sums = Stream(sources, wide_s, narrow_s, in_s)
    ready = Stream(sources, wide_r, narrow_r, in_r)

    barrier = pltpu.get_barrier_semaphore()
    sums.prime(0, experts)
    for peer in peers:
        pl.semaphore_signal(barrier, inc=1, device_id={"fsdp": peer}, device_id_type=MESH)
    for twin in twins:
        pl.semaphore_signal(barrier, inc=1, device_id={"ep": twin}, device_id_type=MESH)

    def push(src, dst, axis, target, s, r):
        pltpu.make_async_remote_copy(
            src_ref=src, dst_ref=dst, send_sem=s, recv_sem=r,
            device_id={axis: target}, device_id_type=MESH,
        ).start()

    def sums_0(e, m, wide, narrow):
        row_sums(wide, narrow, land_0.at[me], pl.ds(m, 1))

    def sums_a(e, m, wide, narrow):
        row_sums(wide, narrow, part_a.at[(e - first) * 2 + m], pl.ds(0, 1))

    share = part_z.shape[1]

    def sums_z(e, m, wide, narrow):
        at = (e - second) * 2 + m
        row_sums(wide, narrow, part_z.at[at // share], pl.ds(at % share, 1))

    def keep(e, m, total):
        scales[m][pl.ds(e, 1), :] = total / (n * depth)

    begin_0 = sender(n, me, peers, send, scales, readys, 0, own_sem.at[0], send_sem.at[0], recv_sem.at[0])
    begin_1 = sender(n, me, peers, send, scales, readys, 0, own_sem.at[1], send_sem.at[1], recv_sem.at[1])

    sums.one(0, experts, sums_0)
    pl.semaphore_wait(barrier, n - 1 + p - 1)
    for peer in peers:
        push(land_0.at[me], land_0.at[me], "fsdp", peer, small_send.at[0], small_recv.at[0])
    ready.prime(0, stop)
    sums.run(first, second, experts, sums_a)
    for peer in peers:
        push(part_a.at[peer], land_a.at[me], "fsdp", peer, small_send.at[1], small_recv.at[1])
    land_a[me] = part_a[me]
    drain(land_0.at[pl.ds(0, n - 1)], small_recv.at[0])
    total_0 = jnp.sum(land_0[...], axis=0)
    for m in range(2):
        keep(0, m, total_0[m:m + 1])
    ready.one(0, stop, begin_0)
    drain(land_a.at[pl.ds(0, n - 1)], small_recv.at[1])
    tot_a[me] = jnp.sum(land_a[...], axis=0)
    for peer in peers:
        push(tot_a.at[me], tot_a.at[me], "fsdp", peer, small_send.at[2], small_recv.at[2])
    rows_r[me] = (rw[...] * rgain[...]).astype(bf16)
    push(rows_r.at[me], rows_r.at[me], "fsdp", far, r_send.at[0], r_recv.at[0])
    some = second + (experts - second) * 2 // 5
    sums.run(second, some, experts, sums_z)
    drain(tot_a.at[pl.ds(0, n - 1)], small_recv.at[2])
    for k in range(n):
        keep(first + k // 2, k % 2, tot_a[k])
    ready.run(1, 2, stop, begin_0)
    sums.run(some, experts, experts, sums_z)
    spare = half * share - 2 * (experts - second)
    if spare:
        part_z[half - 1, share - spare:, :] = jnp.zeros((spare, width), f32)
    for peer, at in zip(near, near_at):
        push(part_z.at[at], land_z.at[mine], "fsdp", peer, small_send.at[3], small_recv.at[3])
    land_z[mine] = part_z[mine]
    ready.run(2, 3, stop, begin_0)
    drain(land_z.at[pl.ds(0, half - 1)], small_recv.at[3])
    sum_z[...] = jnp.sum(land_z[...], axis=0)
    push(sum_z, far_z, "fsdp", far, small_send.at[4], small_recv.at[4])
    drain(rows_r.at[0], r_recv.at[0])
    for peer in near:
        push(rows_r.at[me], rows_r.at[me], "fsdp", peer, r_send.at[1], r_recv.at[1])
        push(rows_r.at[far], rows_r.at[far], "fsdp", peer, r_send.at[1], r_recv.at[1])
    ready.run(3, 4, stop, begin_0)
    drain(far_z, small_recv.at[4])
    tot_z[mine] = sum_z[...] + far_z[...]
    for peer in near:
        push(tot_z.at[mine], tot_z.at[mine], "fsdp", peer, small_send.at[5], small_recv.at[5])
    ready.run(4, second, stop, begin_0)
    drain(tot_z.at[pl.ds(0, half - 1)], small_recv.at[5])

    def keep_z(i, _):
        for m in range(2):
            at = i * 2 + m
            keep(second + i, m, tot_z[at // share, pl.ds(at % share, 1), :])
        return 0

    lax.fori_loop(0, experts - second, keep_z, 0)
    ready.run(second, cut, stop, begin_0)
    ready.run(cut, stop, stop, begin_1)
    drain(rows_r.at[pl.ds(0, n - 2)], r_recv.at[1])
    for twin in twins:
        push(rows_r, all_r.at[group], "ep", twin, r_send.at[2], r_recv.at[2])
    all_r[group] = rows_r[...]
    if p > 1:
        drain(all_r.at[pl.ds(0, p - 1)], r_recv.at[2])
    for f in range(n):
        block = all_r[:, f].astype(f32)
        block = block.reshape(block.shape[0] * block.shape[1], depth)
        router[f * depth:(f + 1) * depth, :] = block.T.astype(bf16)
    drain(land_0.at[pl.ds(0, n - 1)], small_send.at[0])
    drain(part_a.at[pl.ds(0, n - 1)], small_send.at[1])
    drain(tot_a.at[pl.ds(0, n - 1)], small_send.at[2])
    drain(part_z.at[pl.ds(0, half - 1)], small_send.at[3])
    drain(sum_z, small_send.at[4])
    drain(tot_z.at[pl.ds(0, half - 1)], small_send.at[5])
    drain(rows_r.at[0], r_send.at[0])
    drain(rows_r.at[pl.ds(0, n - 2)], r_send.at[1])
    if p > 1:
        drain(all_r.at[pl.ds(0, p - 1)], r_send.at[2])
    finish(n, cut, send, readys, own_sem.at[0], send_sem.at[0], recv_sem.at[0])

    @pl.when(odd)
    def _():
        finish(n, more, send, readys, own_sem.at[1], send_sem.at[1], recv_sem.at[1])


def rest_kernel(n, cut, more, tg, og, tu, ou, scale_gate, scale_up, ready_gate, ready_up,
                wide, narrow, send, in_sem, send_sem, recv_sem):
    experts = tg.shape[0]
    me = lax.axis_index("fsdp")
    odd = lax.rem(lax.axis_index("ep"), 2) == 1
    start = jnp.where(odd, cut + more, cut)
    readys, scales = (ready_gate, ready_up), (scale_gate, scale_up)
    peers = [(me + d) % n for d in far_first(n)]
    ready = Stream(((tg, og), (tu, ou)), wide, narrow, in_sem)
    barrier = pltpu.get_barrier_semaphore()
    for peer in peers:
        pl.semaphore_signal(barrier, inc=1, device_id={"fsdp": peer}, device_id_type=MESH)
    ready.prime(start, experts)
    pl.semaphore_wait(barrier, n - 1)
    begin = [
        sender(n, me, peers, send, scales, readys, cut, None, send_sem.at[k], recv_sem.at[k])
        for k in range(2)
    ]
    ready.run(start, cut + more, experts, begin[1])
    ready.run(cut + more, experts, experts, begin[0])
    finish(n, experts - cut - more, send, readys, None, send_sem.at[0], recv_sem.at[0])

    @pl.when(jnp.logical_not(odd))
    def _():
        finish(n, more, send, readys, None, send_sem.at[1], recv_sem.at[1])


def copy_through(pairs, count, buffer, in_sem, out_sem):
    def bring(i, k):
        slot = lax.rem(i, RING)
        return pltpu.make_async_copy(pairs[k][0].at[i], buffer.at[k, slot], in_sem.at[k, slot])

    def give(i, k):
        slot = lax.rem(i, RING)
        return pltpu.make_async_copy(buffer.at[k, slot], pairs[k][1].at[i], out_sem.at[k, slot])

    def opening(i, _):
        for k in range(2):
            bring(i, k).start()
        return 0

    lax.fori_loop(0, jnp.minimum(count, RING), opening, 0)

    def step(i, _):
        @pl.when(i < count)
        def _():
            for k in range(2):
                bring(i, k).wait()
                give(i, k).start()

        @pl.when(i >= LAG)
        def _():
            for k in range(2):
                give(i - LAG, k).wait()

            @pl.when(i - LAG + RING < count)
            def _():
                for k in range(2):
                    bring(i - LAG + RING, k).start()

        return 0

    lax.fori_loop(0, count + LAG, step, 0)


def own_columns(n, scale, out):
    me = lax.axis_index("fsdp")
    piece = out.shape[1]
    value = jnp.zeros(out.shape, out.dtype)
    for j in range(n):
        value = jnp.where(me == j, scale[:, j * piece:(j + 1) * piece], value)
    out[...] = value


def place_kernel(n, cut, more, got_gate, got_up, scale_gate, scale_up, router,
                 gate, up, own_gate, own_up, full_gate, full_up, router_out, buffer, in_sem, out_sem):
    odd = lax.rem(lax.axis_index("ep"), 2) == 1
    high = jnp.where(odd, cut + more, cut)
    copy_through(((got_gate, gate), (got_up, up)), high, buffer, in_sem, out_sem)
    own_columns(n, scale_gate, own_gate)
    own_columns(n, scale_up, own_up)
    full_gate[...] = scale_gate[...]
    full_up[...] = scale_up[...]
    router_out[...] = router[...]


def end_kernel(n, cut, more, got_gate, got_up, had_gate, had_up, gate, up, sem):
    odd = lax.rem(lax.axis_index("ep"), 2) == 1
    experts = gate.shape[0]
    early, late = pl.ds(0, more), pl.ds(more, experts - cut - more)

    def copies(some, low, count, k):
        return [
            pltpu.make_async_copy(got.at[some], out.at[pl.ds(low, count)], sem.at[k, m])
            for m, (got, out) in enumerate(((got_gate, gate), (got_up, up)))
        ]

    both = copies(late, cut + more, experts - cut - more, 0)
    for copy in both:
        copy.start()

    @pl.when(jnp.logical_not(odd))
    def _():
        others = copies(early, cut, more, 1)
        for copy in others:
            copy.start()
        for copy in others:
            copy.wait()

    for copy in both:
        copy.wait()


def sending_device(n, p, train_gate, other_gate, train_up, other_up, router_weight, router_gain):
    experts, depth, width = train_gate.shape
    piece = width // n
    columns = router_weight.shape[1]
    half = n // 2
    share = -(-2 * (experts - 1 - half) // half)
    tail = experts // 16
    more = experts // 8
    cut = experts - tail - more
    bulk, rest = cut + more, experts - cut
    anywhere = pl.BlockSpec(memory_space=pltpu.HBM)
    vmem = pl.BlockSpec(memory_space=pltpu.VMEM)
    shape = jax.ShapeDtypeStruct
    full = shape((experts, width), f32)
    own = shape((experts, piece), f32)
    whole = shape((experts, piece, n * depth), bf16)
    routed = shape((n * depth, p * columns), bf16)
    dma = pltpu.SemaphoreType.DMA
    got_gate, got_up, scale_gate, scale_up, router = pl.pallas_call(
        functools.partial(bulk_kernel, n, p, cut, more),
        out_shape=(shape((bulk, piece, n * depth), bf16),) * 2 + (full, full, routed),
        in_specs=[anywhere] * 4 + [vmem] * 2,
        out_specs=(anywhere, anywhere, vmem, vmem, vmem),
        scratch_shapes=[
            pltpu.VMEM((2, SLOTS, depth, width), f32),
            pltpu.VMEM((2, SLOTS, depth, width), bf16),
            pltpu.VMEM((2, SLOTS, depth, width), f32),
            pltpu.VMEM((2, SLOTS, depth, width), bf16),
            pltpu.VMEM((2, bulk, width, depth), bf16),
            pltpu.VMEM((n, 2, width), f32),
            *[pltpu.VMEM((n, 1, width), f32)] * 3,
            *[pltpu.VMEM((half, share, width), f32)] * 2,
            *[pltpu.VMEM((share, width), f32)] * 2,
            pltpu.VMEM((half, share, width), f32),
            pltpu.VMEM((n, columns, depth), bf16),
            pltpu.VMEM((p, n, columns, depth), bf16),
            dma((2, 2, SLOTS)), dma((2, 2, SLOTS)), dma((2, 2)), dma((2, 2)), dma((2, 2)),
            dma((6,)), dma((6,)), dma((3,)), dma((3,)),
        ],
        compiler_params=pltpu.CompilerParams(
            collective_id=0, has_side_effects=True, vmem_limit_bytes=60 * 2**20
        ),
        name="send_bulk",
    )(train_gate, other_gate, train_up, other_up, router_weight.T, router_gain[None, :])
    ring = [pltpu.VMEM((2, RING, piece, n * depth), bf16), dma((2, RING)), dma((2, RING))]
    gate, up, own_gate, own_up, scale_gate, scale_up, router = pl.pallas_call(
        functools.partial(place_kernel, n, cut, more),
        out_shape=(whole, whole, own, own, full, full, routed),
        in_specs=[anywhere] * 2 + [vmem] * 3,
        out_specs=(anywhere, anywhere, vmem, vmem, vmem, vmem, vmem),
        scratch_shapes=ring,
        compiler_params=pltpu.CompilerParams(vmem_limit_bytes=40 * 2**20),
        name="place_bulk",
    )(got_gate, got_up, scale_gate, scale_up, router)
    got_gate, got_up = pl.pallas_call(
        functools.partial(rest_kernel, n, cut, more),
        out_shape=(shape((rest, piece, n * depth), bf16),) * 2,
        in_specs=[anywhere] * 4 + [vmem] * 2,
        out_specs=(vmem, vmem),
        scratch_shapes=[
            pltpu.VMEM((2, SLOTS, depth, width), f32),
            pltpu.VMEM((2, SLOTS, depth, width), bf16),
            pltpu.VMEM((2, rest, width, depth), bf16),
            dma((2, 2, SLOTS)), dma((2, 2)), dma((2, 2)),
        ],
        compiler_params=pltpu.CompilerParams(
            collective_id=1, has_side_effects=True, vmem_limit_bytes=40 * 2**20
        ),
        name="send_rest",
    )(train_gate, other_gate, train_up, other_up, scale_gate, scale_up)
    gate, up = pl.pallas_call(
        functools.partial(end_kernel, n, cut, more),
        out_shape=(whole, whole),
        in_specs=[vmem] * 2 + [anywhere] * 2,
        out_specs=(anywhere, anywhere),
        scratch_shapes=[dma((2, 2))],
        input_output_aliases={2: 0, 3: 1},
        compiler_params=pltpu.CompilerParams(vmem_limit_bytes=40 * 2**20),
        name="place_rest",
    )(got_gate, got_up, gate, up)
    return (jnp.swapaxes(gate, 1, 2), jnp.swapaxes(up, 1, 2), own_gate, own_up, router)


def solution(mesh):
    n, p = mesh.shape["fsdp"], mesh.shape["ep"]

    def per_device(*args):
        experts, depth, width = args[0].shape
        fits = (
            depth % 128 == 0 and width % (16 * n) == 0 and width % 128 == 0 and n % 4 == 0
            and experts % 16 == 0 and experts >= n + 8 and args[4].shape[1] % 16 == 0
            and 2 * experts * depth * width * 2 <= 2**25
        )
        return sending_device(n, p, *args) if fits else plain_device(*args)

    matrix = P("ep", "fsdp", None)
    in_specs = (matrix, matrix, matrix, matrix, P("fsdp", "ep"), P("fsdp"))
    out_specs = (P("ep", None, "fsdp"), P("ep", None, "fsdp"), P("ep", "fsdp"), P("ep", "fsdp"), P())
    return jax.shard_map(
        per_device, mesh=mesh, in_specs=in_specs, out_specs=out_specs, check_vma=False
    )
```

time: 591 us -> 570 us (0.964)
  local copies, waits for them, and re-layouts: 20 us -> 7.17 us
  Pallas kernels: 570 us -> 562 us
    unnamed x7 -> x8, local copies, waits for them, and re-layouts: 18.5 us -> 7.17 us
    pallas_call x1 -> x4, Pallas kernels: 570 us -> 562 us  [the longest x1 473 us: sending_device(): pl.pallas_call(functools.partial(bulk_kernel, n, p, cut, more), out_shape...]
where the time goes in v1:
time: 570 us
  Pallas kernels  562 us (99%)
  local copies, waits for them, and re-layouts  7.17 us (1%)
    pallas_call x1, Pallas kernels, sending_device(): pl.pallas_call(functools.partial(bulk_kernel, n, p, cut, more), out_shape...  473 us
    pallas_call x1, Pallas kernels, sending_device(): pl.pallas_call(functools.partial(rest_kernel, n, cut, more), out_shape=(s...  72.9 us
    pallas_call x1, Pallas kernels, sending_device(): pl.pallas_call(functools.partial(place_kernel, n, cut, more), out_shape=(...  13.2 us

profile of v1, /device:TPU:0, one launch (start us, length us, event | category | flops | bytes accessed | tf_op | source)
XLA Modules:
  0.0 569.5 jit_solution(5797692016127765417)
XLA Ops:
  0.6 473.3 %send_bulk.1 = (bf16[30,96,2048]{2,1,0:T(8,128)(2,1)}, bf16[30,96,2048]{2,1,0:T(8,128)(2,1)}, f32[32,768]{1,0:T(8,128)}, f32[32,768]{1,0:T(8,128)}, bf16[2048,128]{1,0:T(8,128)(2,1)}) custom-call(f32[32,256,768]{2,1,0:T(8,128)} %tg.3, bf16[32,256,768]{2,1,0:T(8,128)(2,1)} %og.3, f32[32,256,768]{2,1,0:T(8,128)} %tu.3, bf16[32,256,768]{2,1,0:T(8,128)(2,1)} %ou.3, ...), custom_call_target="tpu_custom_call" | custom-call | tf_op jit(solution)/shard_map/send_bulk/pallas_call | solution.py:408
  474.0 0.0 copy-start
  474.0 4.3 copy-done
  478.3 0.0 copy-start.1
  478.3 1.0 copy-done.1
  479.4 0.0 copy-start.2
  479.4 0.9 copy-done.2
  480.2 0.0 copy-start.3
  480.3 0.9 copy-done.3
  481.1 13.2 %place_bulk.1 = (bf16[32,96,2048]{2,1,0:T(8,128)(2,1)}, bf16[32,96,2048]{2,1,0:T(8,128)(2,1)}, f32[32,96]{1,0:T(8,128)}, f32[32,96]{1,0:T(8,128)}, f32[32,768]{1...) custom-call(bf16[30,96,2048]{2,1,0:T(8,128)(2,1)S(1)} %copy-done, ...), custom_call_target="tpu_custom_call" | custom-call | tf_op jit(solution)/shard_map/place_bulk/pallas_call | solution.py:435
  494.3 72.9 %send_rest.1 = (bf16[6,96,2048]{2,1,0:T(8,128)(2,1)S(1)}, bf16[6,96,2048]{2,1,0:T(8,128)(2,1)S(1)}) custom-call(f32[32,256,768]{2,1,0:T(8,128)} %tg.3, bf16[32,256,768]{2,1,0:T(8,128)(2,1)} %og.3, f32[32,256,768]{2,1,0:T(8,128)} %tu.3, bf16[32,256,768]{2,1,0:T(8,128)(2,1)} %ou.3, f32[32,768]{1,0:T(8,128)S(1)} %get-tuple-element.26.scale_gate, ...), custom_call_target="tpu_custom_call" | custom-call | tf_op jit(solution)/shard_map/send_rest/pallas_call | solution.py:444
  567.3 2.2 place_rest.1
Async XLA Ops:
  474.0 4.4 copy-start
  478.3 1.0 copy-start.1
  479.4 0.9 copy-start.2
  480.2 0.9 copy-start.3

commit v2 on v1

--- a/solution.py
+++ b/solution.py
@@ -9,8 +9,8 @@
 
 MESH = pl.DeviceIdType.MESH
 SLOTS = 3
-RING = 8
-LAG = 4
+RING = 20
+SLOW = 2
 f32, bf16 = jnp.float32, jnp.bfloat16
 
 
@@ -172,7 +172,11 @@
         ).start()
 
     def sums_0(e, m, wide, narrow):
-        row_sums(wide, narrow, land_0.at[me], pl.ds(m, 1))
+        row_sums(wide, narrow, land_0.at[m, me], pl.ds(0, 1))
+        if m == 0:
+            pl.semaphore_wait(barrier, n - 1 + p - 1)
+        for peer in peers:
+            push(land_0.at[m, me], land_0.at[m, me], "fsdp", peer, small_send.at[m], small_recv.at[m])
 
     def sums_a(e, m, wide, narrow):
         row_sums(wide, narrow, part_a.at[(e - first) * 2 + m], pl.ds(0, 1))
@@ -189,29 +193,28 @@
     begin_0 = sender(n, me, peers, send, scales, readys, 0, own_sem.at[0], send_sem.at[0], recv_sem.at[0])
     begin_1 = sender(n, me, peers, send, scales, readys, 0, own_sem.at[1], send_sem.at[1], recv_sem.at[1])
 
+    def begin_first(e, m, wide, narrow):
+        drain(land_0.at[m, pl.ds(0, n - 1)], small_recv.at[m])
+        keep(e, m, jnp.sum(land_0[m], axis=0))
+        if m == 1:
+            drain(land_a.at[pl.ds(0, n - 1)], small_recv.at[2])
+            tot_a[me] = jnp.sum(land_a[...], axis=0)
+            for peer in peers:
+                push(tot_a.at[me], tot_a.at[me], "fsdp", peer, small_send.at[3], small_recv.at[3])
+        begin_0(e, m, wide, narrow)
+
     sums.one(0, experts, sums_0)
-    pl.semaphore_wait(barrier, n - 1 + p - 1)
-    for peer in peers:
-        push(land_0.at[me], land_0.at[me], "fsdp", peer, small_send.at[0], small_recv.at[0])
+    rows_r[me] = (rw[...] * rgain[...]).astype(bf16)
+    push(rows_r.at[me], rows_r.at[me], "fsdp", far, r_send.at[0], r_recv.at[0])
     ready.prime(0, stop)
     sums.run(first, second, experts, sums_a)
     for peer in peers:
-        push(part_a.at[peer], land_a.at[me], "fsdp", peer, small_send.at[1], small_recv.at[1])
+        push(part_a.at[peer], land_a.at[me], "fsdp", peer, small_send.at[2], small_recv.at[2])
     land_a[me] = part_a[me]
-    drain(land_0.at[pl.ds(0, n - 1)], small_recv.at[0])
-    total_0 = jnp.sum(land_0[...], axis=0)
-    for m in range(2):
-        keep(0, m, total_0[m:m + 1])
-    ready.one(0, stop, begin_0)
-    drain(land_a.at[pl.ds(0, n - 1)], small_recv.at[1])
-    tot_a[me] = jnp.sum(land_a[...], axis=0)
-    for peer in peers:
-        push(tot_a.at[me], tot_a.at[me], "fsdp", peer, small_send.at[2], small_recv.at[2])
-    rows_r[me] = (rw[...] * rgain[...]).astype(bf16)
-    push(rows_r.at[me], rows_r.at[me], "fsdp", far, r_send.at[0], r_recv.at[0])
+    ready.one(0, stop, begin_first)
     some = second + (experts - second) * 2 // 5
     sums.run(second, some, experts, sums_z)
-    drain(tot_a.at[pl.ds(0, n - 1)], small_recv.at[2])
+    drain(tot_a.at[pl.ds(0, n - 1)], small_recv.at[3])
     for k in range(n):
         keep(first + k // 2, k % 2, tot_a[k])
     ready.run(1, 2, stop, begin_0)
@@ -220,23 +223,23 @@
     if spare:
         part_z[half - 1, share - spare:, :] = jnp.zeros((spare, width), f32)
     for peer, at in zip(near, near_at):
-        push(part_z.at[at], land_z.at[mine], "fsdp", peer, small_send.at[3], small_recv.at[3])
+        push(part_z.at[at], land_z.at[mine], "fsdp", peer, small_send.at[4], small_recv.at[4])
     land_z[mine] = part_z[mine]
     ready.run(2, 3, stop, begin_0)
-    drain(land_z.at[pl.ds(0, half - 1)], small_recv.at[3])
+    drain(land_z.at[pl.ds(0, half - 1)], small_recv.at[4])
     sum_z[...] = jnp.sum(land_z[...], axis=0)
-    push(sum_z, far_z, "fsdp", far, small_send.at[4], small_recv.at[4])
+    push(sum_z, far_z, "fsdp", far, small_send.at[5], small_recv.at[5])
     drain(rows_r.at[0], r_recv.at[0])
     for peer in near:
         push(rows_r.at[me], rows_r.at[me], "fsdp", peer, r_send.at[1], r_recv.at[1])
         push(rows_r.at[far], rows_r.at[far], "fsdp", peer, r_send.at[1], r_recv.at[1])
     ready.run(3, 4, stop, begin_0)
-    drain(far_z, small_recv.at[4])
+    drain(far_z, small_recv.at[5])
     tot_z[mine] = sum_z[...] + far_z[...]
     for peer in near:
-        push(tot_z.at[mine], tot_z.at[mine], "fsdp", peer, small_send.at[5], small_recv.at[5])
+        push(tot_z.at[mine], tot_z.at[mine], "fsdp", peer, small_send.at[6], small_recv.at[6])
     ready.run(4, second, stop, begin_0)
-    drain(tot_z.at[pl.ds(0, half - 1)], small_recv.at[5])
+    drain(tot_z.at[pl.ds(0, half - 1)], small_recv.at[6])
 
     def keep_z(i, _):
         for m in range(2):
@@ -257,12 +260,13 @@
         block = all_r[:, f].astype(f32)
         block = block.reshape(block.shape[0] * block.shape[1], depth)
         router[f * depth:(f + 1) * depth, :] = block.T.astype(bf16)
-    drain(land_0.at[pl.ds(0, n - 1)], small_send.at[0])
-    drain(part_a.at[pl.ds(0, n - 1)], small_send.at[1])
-    drain(tot_a.at[pl.ds(0, n - 1)], small_send.at[2])
-    drain(part_z.at[pl.ds(0, half - 1)], small_send.at[3])
-    drain(sum_z, small_send.at[4])
-    drain(tot_z.at[pl.ds(0, half - 1)], small_send.at[5])
+    for m in range(2):
+        drain(land_0.at[m, pl.ds(0, n - 1)], small_send.at[m])
+    drain(part_a.at[pl.ds(0, n - 1)], small_send.at[2])
+    drain(tot_a.at[pl.ds(0, n - 1)], small_send.at[3])
+    drain(part_z.at[pl.ds(0, half - 1)], small_send.at[4])
+    drain(sum_z, small_send.at[5])
+    drain(tot_z.at[pl.ds(0, half - 1)], small_send.at[6])
     drain(rows_r.at[0], r_send.at[0])
     drain(rows_r.at[pl.ds(0, n - 2)], r_send.at[1])
     if p > 1:
@@ -274,7 +278,7 @@
         finish(n, more, send, readys, own_sem.at[1], send_sem.at[1], recv_sem.at[1])
 
 
-def rest_kernel(n, cut, more, tg, og, tu, ou, scale_gate, scale_up, ready_gate, ready_up,
+def rest_kernel(n, cut, more, tg, og, tu, ou, scale_gate, scale_up, placed, ready_gate, ready_up,
                 wide, narrow, send, in_sem, send_sem, recv_sem):
     experts = tg.shape[0]
     me = lax.axis_index("fsdp")
@@ -301,13 +305,15 @@
         finish(n, more, send, readys, None, send_sem.at[1], recv_sem.at[1])
 
 
-def copy_through(pairs, count, buffer, in_sem, out_sem):
+def copy_through(pairs, count, deep, buffer, in_sem, out_sem):
+    lag = deep // 2
+
     def bring(i, k):
-        slot = lax.rem(i, RING)
+        slot = lax.rem(i, deep)
         return pltpu.make_async_copy(pairs[k][0].at[i], buffer.at[k, slot], in_sem.at[k, slot])
 
     def give(i, k):
-        slot = lax.rem(i, RING)
+        slot = lax.rem(i, deep)
         return pltpu.make_async_copy(buffer.at[k, slot], pairs[k][1].at[i], out_sem.at[k, slot])
 
     def opening(i, _):
@@ -315,7 +321,7 @@
             bring(i, k).start()
         return 0
 
-    lax.fori_loop(0, jnp.minimum(count, RING), opening, 0)
+    lax.fori_loop(0, jnp.minimum(count, deep), opening, 0)
 
     def step(i, _):
         @pl.when(i < count)
@@ -324,19 +330,19 @@
                 bring(i, k).wait()
                 give(i, k).start()
 
-        @pl.when(i >= LAG)
+        @pl.when(i >= lag)
         def _():
             for k in range(2):
-                give(i - LAG, k).wait()
-
-            @pl.when(i - LAG + RING < count)
+                give(i - lag, k).wait()
+
+            @pl.when(i - lag + deep < count)
             def _():
                 for k in range(2):
-                    bring(i - LAG + RING, k).start()
+                    bring(i - lag + deep, k).start()
 
         return 0
 
-    lax.fori_loop(0, count + LAG, step, 0)
+    lax.fori_loop(0, count + lag, step, 0)
 
 
 def own_columns(n, scale, out):
@@ -349,15 +355,22 @@
 
 
 def place_kernel(n, cut, more, got_gate, got_up, scale_gate, scale_up, router,
-                 gate, up, own_gate, own_up, full_gate, full_up, router_out, buffer, in_sem, out_sem):
+                 gate, up, own_gate, own_up, router_out, buffer, scales, in_sem, out_sem, small_sem):
     odd = lax.rem(lax.axis_index("ep"), 2) == 1
     high = jnp.where(odd, cut + more, cut)
-    copy_through(((got_gate, gate), (got_up, up)), high, buffer, in_sem, out_sem)
-    own_columns(n, scale_gate, own_gate)
-    own_columns(n, scale_up, own_up)
-    full_gate[...] = scale_gate[...]
-    full_up[...] = scale_up[...]
-    router_out[...] = router[...]
+    small = [
+        pltpu.make_async_copy(scale_gate, scales.at[0], small_sem.at[0]),
+        pltpu.make_async_copy(scale_up, scales.at[1], small_sem.at[1]),
+        pltpu.make_async_copy(router, router_out, small_sem.at[2]),
+    ]
+    for copy in small:
+        copy.start()
+    deep = jnp.where(odd, SLOW, RING)
+    copy_through(((got_gate, gate), (got_up, up)), high, deep, buffer, in_sem, out_sem)
+    for copy in small:
+        copy.wait()
+    own_columns(n, scales[0], own_gate)
+    own_columns(n, scales[1], own_up)
 
 
 def end_kernel(n, cut, more, got_gate, got_up, had_gate, had_up, gate, up, sem):
@@ -393,8 +406,8 @@
     columns = router_weight.shape[1]
     half = n // 2
     share = -(-2 * (experts - 1 - half) // half)
-    tail = experts // 16
-    more = experts // 8
+    tail = experts // 32
+    more = 3 * experts // 16
     cut = experts - tail - more
     bulk, rest = cut + more, experts - cut
     anywhere = pl.BlockSpec(memory_space=pltpu.HBM)
@@ -416,7 +429,7 @@
             pltpu.VMEM((2, SLOTS, depth, width), f32),
             pltpu.VMEM((2, SLOTS, depth, width), bf16),
             pltpu.VMEM((2, bulk, width, depth), bf16),
-            pltpu.VMEM((n, 2, width), f32),
+            pltpu.VMEM((2, n, 1, width), f32),
             *[pltpu.VMEM((n, 1, width), f32)] * 3,
             *[pltpu.VMEM((half, share, width), f32)] * 2,
             *[pltpu.VMEM((share, width), f32)] * 2,
@@ -424,27 +437,30 @@
             pltpu.VMEM((n, columns, depth), bf16),
             pltpu.VMEM((p, n, columns, depth), bf16),
             dma((2, 2, SLOTS)), dma((2, 2, SLOTS)), dma((2, 2)), dma((2, 2)), dma((2, 2)),
-            dma((6,)), dma((6,)), dma((3,)), dma((3,)),
+            dma((7,)), dma((7,)), dma((3,)), dma((3,)),
         ],
         compiler_params=pltpu.CompilerParams(
             collective_id=0, has_side_effects=True, vmem_limit_bytes=60 * 2**20
         ),
         name="send_bulk",
     )(train_gate, other_gate, train_up, other_up, router_weight.T, router_gain[None, :])
-    ring = [pltpu.VMEM((2, RING, piece, n * depth), bf16), dma((2, RING)), dma((2, RING))]
-    gate, up, own_gate, own_up, scale_gate, scale_up, router = pl.pallas_call(
+    gate, up, own_gate, own_up, router = pl.pallas_call(
         functools.partial(place_kernel, n, cut, more),
-        out_shape=(whole, whole, own, own, full, full, routed),
-        in_specs=[anywhere] * 2 + [vmem] * 3,
-        out_specs=(anywhere, anywhere, vmem, vmem, vmem, vmem, vmem),
-        scratch_shapes=ring,
-        compiler_params=pltpu.CompilerParams(vmem_limit_bytes=40 * 2**20),
+        out_shape=(whole, whole, own, own, routed),
+        in_specs=[anywhere] * 5,
+        out_specs=(anywhere, anywhere, vmem, vmem, vmem),
+        scratch_shapes=[
+            pltpu.VMEM((2, RING, piece, n * depth), bf16),
+            pltpu.VMEM((2, experts, width), f32),
+            dma((2, RING)), dma((2, RING)), dma((3,)),
+        ],
+        compiler_params=pltpu.CompilerParams(vmem_limit_bytes=60 * 2**20),
         name="place_bulk",
     )(got_gate, got_up, scale_gate, scale_up, router)
     got_gate, got_up = pl.pallas_call(
         functools.partial(rest_kernel, n, cut, more),
         out_shape=(shape((rest, piece, n * depth), bf16),) * 2,
-        in_specs=[anywhere] * 4 + [vmem] * 2,
+        in_specs=[anywhere] * 4 + [vmem] * 2 + [anywhere],
         out_specs=(vmem, vmem),
         scratch_shapes=[
             pltpu.VMEM((2, SLOTS, depth, width), f32),
@@ -456,7 +472,7 @@
             collective_id=1, has_side_effects=True, vmem_limit_bytes=40 * 2**20
         ),
         name="send_rest",
-    )(train_gate, other_gate, train_up, other_up, scale_gate, scale_up)
+    )(train_gate, other_gate, train_up, other_up, scale_gate, scale_up, own_gate)
     gate, up = pl.pallas_call(
         functools.partial(end_kernel, n, cut, more),
         out_shape=(whole, whole),
@@ -477,7 +493,7 @@
         experts, depth, width = args[0].shape
         fits = (
             depth % 128 == 0 and width % (16 * n) == 0 and width % 128 == 0 and n % 4 == 0
-            and experts % 16 == 0 and experts >= n + 8 and args[4].shape[1] % 16 == 0
+            and experts % 32 == 0 and experts >= n + 8 and args[4].shape[1] % 16 == 0
             and 2 * experts * depth * width * 2 <= 2**25
         )
         return sending_device(n, p, *args) if fits else plain_device(*args)

time: 570 us -> 556 us (0.975); the launches traced: 570 us -> 549 us
  Pallas kernels: 562 us -> 548 us
  local copies, waits for them, and re-layouts: 7.17 us -> 0.72 us
    pallas_call x1, Pallas kernels: 473 us -> 463 us  [sending_device(): pl.pallas_call(functools.partial(bulk_kernel, n, p, cut, more), out_shape...]
    unnamed x8 -> x6, local copies, waits for them, and re-layouts: 7.17 us -> 0.72 us
where the time goes in v2:
time: 556 us; the launch traced here: 549 us
  Pallas kernels  548 us (99%)
    pallas_call x1, Pallas kernels, sending_device(): pl.pallas_call(functools.partial(bulk_kernel, n, p, cut, more), out_shape...  463 us
    pallas_call x1, Pallas kernels, sending_device(): pl.pallas_call(functools.partial(rest_kernel, n, cut, more), out_shape=(s...  67.3 us
    pallas_call x1, Pallas kernels, sending_device(): pl.pallas_call(functools.partial(place_kernel, n, cut, more), out_shape=(...  15.7 us

profile of v2, /device:TPU:0, one launch (start us, length us, event | category | flops | bytes accessed | tf_op | source)
XLA Modules:
  0.0 549.5 jit_solution(6541024264631229014)
XLA Ops:
  0.6 462.5 %send_bulk.1 = (bf16[31,96,2048]{2,1,0:T(8,128)(2,1)}, bf16[31,96,2048]{2,1,0:T(8,128)(2,1)}, f32[32,768]{1,0:T(8,128)}, f32[32,768]{1,0:T(8,128)}, bf16[2048,128]{1,0:T(8,128)(2,1)}) custom-call(f32[32,256,768]{2,1,0:T(8,128)} %tg.3, bf16[32,256,768]{2,1,0:T(8,128)(2,1)} %og.3, f32[32,256,768]{2,1,0:T(8,128)} %tu.3, bf16[32,256,768]{2,1,0:T(8,128)(2,1)} %ou.3, ...), custom_call_target="tpu_custom_call" | custom-call | tf_op jit(solution)/shard_map/send_bulk/pallas_call | solution.py:421
  463.2 0.0 copy-start
  463.2 0.0 copy-start.1
  463.2 15.7 %place_bulk.1 = (bf16[32,96,2048]{2,1,0:T(8,128)(2,1)}, bf16[32,96,2048]{2,1,0:T(8,128)(2,1)}, f32[32,96]{1,0:T(8,128)}, f32[32,96]{1,0:T(8,128)}, bf16[2048,128]{1,0:T(8,128)(2,1)}) custom-call(bf16[31,96,2048]{2,1,0:T(8,128)(2,1)} %get-tuple-element.21.got_gate, bf16[31,96,2048]{2,1,0:T(8,128)(2,1)} %get-tuple-element.22.got_up, ...), custom_call_target="tpu_custom_call" | custom-call | tf_op jit(solution)/shard_map/place_bulk/pallas_call | solution.py:447
  478.9 0.0 copy-done
  478.9 0.0 copy-done.1
  478.9 0.0 copy-start.2
  478.9 0.7 copy-done.2
  479.7 67.3 %send_rest.1 = (bf16[7,96,2048]{2,1,0:T(8,128)(2,1)S(1)}, bf16[7,96,2048]{2,1,0:T(8,128)(2,1)S(1)}) custom-call(f32[32,256,768]{2,1,0:T(8,128)} %tg.3, bf16[32,256,768]{2,1,0:T(8,128)(2,1)} %og.3, f32[32,256,768]{2,1,0:T(8,128)} %tu.3, bf16[32,256,768]{2,1,0:T(8,128)(2,1)} %ou.3, f32[32,768]{1,0:T(8,128)S(1)} %copy-done, f32[32,768]{1,0:T(8,128)S(1)} %copy-done.1, ...), custom_call_target="tpu_custom_call" | custom-call | tf_op jit(solution)/shard_map/send_rest/pallas_call | solution.py:460
  547.0 2.5 place_rest.1
Async XLA Ops:
  463.2 15.7 %copy-start = (f32[32,768]{1,0:T(8,128)S(1)}, f32[32,768]{1,0:T(8,128)}, u32[]{:S(2)}) copy-start(f32[32,768]{1,0:T(8,128)} %get-tuple-element.19.scale_gate) | copy-start | bytes 294916
  463.2 15.7 %copy-start.1 = (f32[32,768]{1,0:T(8,128)S(1)}, f32[32,768]{1,0:T(8,128)}, u32[]{:S(2)}) copy-start(f32[32,768]{1,0:T(8,128)} %get-tuple-element.20.scale_up) | copy-start | bytes 294916
  478.9 0.7 copy-start.2

commit v3 on v2

--- a/solution.py
+++ b/solution.py
@@ -11,6 +11,7 @@
 SLOTS = 3
 RING = 20
 SLOW = 2
+RAW = 2
 f32, bf16 = jnp.float32, jnp.bfloat16
 
 
@@ -135,19 +136,33 @@
         drain(readys[m].at[some, :, pl.ds(0, (n - 1) * depth)], recv_sem.at[m])
 
 
+def coded(value):
+    square = value * value
+    fourth = square * square
+    return (fourth * fourth) * (square * value)
+
+
+def decoded(code):
+    size = jnp.abs(code)
+    root = jnp.exp(jnp.log(jnp.where(size > 0, size, 1.0)) * (1.0 / 11.0))
+    return jnp.where(size > 0, jnp.where(code < 0, -root, root), 0.0)
+
+
 def bulk_kernel(n, p, cut, more, tg, og, tu, ou, rw, rgain, ready_gate, ready_up, scale_gate, scale_up, router,
-                wide_s, narrow_s, wide_r, narrow_r, send, land_0, part_a, land_a, tot_a,
+                wide_s, narrow_s, wide_r, narrow_r, send, raw_land, part_0, land_0, row_0, part_a, land_a, tot_a,
                 part_z, land_z, sum_z, far_z, tot_z, rows_r, all_r,
-                in_s, in_r, own_sem, send_sem, recv_sem, small_send, small_recv, r_send, r_recv):
+                in_s, in_r, own_sem, send_sem, recv_sem, small_send, small_recv, r_send, r_recv,
+                sum_send, sum_recv, raw_send, raw_recv, raw_out):
     experts, depth, width = tg.shape
     half = n // 2
+    piece = width // n
     me = lax.axis_index("fsdp")
     group = lax.axis_index("ep")
     odd = lax.rem(group, 2) == 1
     stop = jnp.where(odd, cut + more, cut)
     mine = lax.rem(me, half)
     side = me - mine
-    first, second = 1, 1 + half
+    first, second = RAW, RAW + half
     readys, scales = (ready_gate, ready_up), (scale_gate, scale_up)
     peers = [(me + d) % n for d in far_first(n)]
     near = [side + lax.rem(mine + d, half) for d in range(1, half)]
@@ -159,11 +174,11 @@
     ready = Stream(sources, wide_r, narrow_r, in_r)
 
     barrier = pltpu.get_barrier_semaphore()
-    sums.prime(0, experts)
     for peer in peers:
         pl.semaphore_signal(barrier, inc=1, device_id={"fsdp": peer}, device_id_type=MESH)
     for twin in twins:
         pl.semaphore_signal(barrier, inc=1, device_id={"ep": twin}, device_id_type=MESH)
+    sums.prime(0, experts)
 
     def push(src, dst, axis, target, s, r):
         pltpu.make_async_remote_copy(
@@ -172,11 +187,44 @@
         ).start()
 
     def sums_0(e, m, wide, narrow):
-        row_sums(wide, narrow, land_0.at[m, me], pl.ds(0, 1))
-        if m == 0:
-            pl.semaphore_wait(barrier, n - 1 + p - 1)
+        u = 2 * e + m
+        row_sums(wide, narrow, row_0, pl.ds(0, 1))
+        row = row_0[...]
+        for j in range(n):
+            part_0[u, j, :, 0:piece] = row[:, j * piece:(j + 1) * piece]
+        inverse = jnp.where(row > 0, depth / row, 0.0)
+        for c in range(0, width, 128):
+            latest = wide[:, c:c + 128] + narrow[:, c:c + 128].astype(f32)
+            send[m, e, c:c + 128, :] = coded(latest * inverse[:, c:c + 128]).T.astype(bf16)
+
+    def push_0(u):
+        e, m = divmod(u, 2)
         for peer in peers:
-            push(land_0.at[m, me], land_0.at[m, me], "fsdp", peer, small_send.at[m], small_recv.at[m])
+            push(part_0.at[u, peer], land_0.at[u, me], "fsdp", peer, sum_send.at[u], sum_recv.at[u])
+        for peer in peers:
+            push(send.at[m, e, pl.ds(pl.multiple_of(peer * piece, 16), piece), :],
+                 raw_land.at[u, :, pl.ds(pl.multiple_of(me * depth, 128), depth)],
+                 "fsdp", peer, raw_send.at[u], raw_recv.at[u])
+
+    def end_0(u):
+        e, m = divmod(u, 2)
+        raw_land[u, :, pl.ds(pl.multiple_of(me * depth, 128), depth)] = (
+            send[m, e, pl.ds(pl.multiple_of(me * piece, 16), piece), :]
+        )
+        land_0[u, me] = part_0[u, me]
+        drain(land_0.at[u, pl.ds(0, n - 1)], sum_recv.at[u])
+        drain(raw_land.at[u, :, pl.ds(0, (n - 1) * depth)], raw_recv.at[u])
+        got = land_0[u].reshape(n, 128)
+        scale = jnp.sum(got, axis=0, keepdims=True) / (n * depth)
+        for j in range(n):
+            scales[m][e:e + 1, j * piece:(j + 1) * piece] = scale[:, 0:piece]
+        used = lax.broadcasted_iota(jnp.int32, (1, 128), 1) < piece
+        factor = (got / depth / jnp.where(used, scale, 1.0)).T
+        for s in range(n):
+            code = raw_land[u, :, s * depth:(s + 1) * depth].astype(f32)
+            value = decoded(code) * factor[0:piece, s:s + 1]
+            raw_land[u, :, s * depth:(s + 1) * depth] = value.astype(bf16)
+        pltpu.make_async_copy(raw_land.at[u], readys[m].at[e], raw_out.at[u]).start()
 
     def sums_a(e, m, wide, narrow):
         row_sums(wide, narrow, part_a.at[(e - first) * 2 + m], pl.ds(0, 1))
@@ -193,31 +241,28 @@
     begin_0 = sender(n, me, peers, send, scales, readys, 0, own_sem.at[0], send_sem.at[0], recv_sem.at[0])
     begin_1 = sender(n, me, peers, send, scales, readys, 0, own_sem.at[1], send_sem.at[1], recv_sem.at[1])
 
-    def begin_first(e, m, wide, narrow):
-        drain(land_0.at[m, pl.ds(0, n - 1)], small_recv.at[m])
-        keep(e, m, jnp.sum(land_0[m], axis=0))
-        if m == 1:
-            drain(land_a.at[pl.ds(0, n - 1)], small_recv.at[2])
-            tot_a[me] = jnp.sum(land_a[...], axis=0)
-            for peer in peers:
-                push(tot_a.at[me], tot_a.at[me], "fsdp", peer, small_send.at[3], small_recv.at[3])
-        begin_0(e, m, wide, narrow)
-
+    part_0[...] = jnp.zeros_like(part_0)
     sums.one(0, experts, sums_0)
+    pl.semaphore_wait(barrier, n - 1 + p - 1)
+    push_0(0)
     rows_r[me] = (rw[...] * rgain[...]).astype(bf16)
-    push(rows_r.at[me], rows_r.at[me], "fsdp", far, r_send.at[0], r_recv.at[0])
-    ready.prime(0, stop)
+    for e in range(1, RAW):
+        sums.one(e, experts, sums_0)
     sums.run(first, second, experts, sums_a)
     for peer in peers:
         push(part_a.at[peer], land_a.at[me], "fsdp", peer, small_send.at[2], small_recv.at[2])
     land_a[me] = part_a[me]
-    ready.one(0, stop, begin_first)
-    some = second + (experts - second) * 2 // 5
+    push(rows_r.at[me], rows_r.at[me], "fsdp", far, r_send.at[0], r_recv.at[0])
+    push_0(1)
+    ready.prime(first, stop)
+    some = second + (experts - second) * 7 // 10
     sums.run(second, some, experts, sums_z)
-    drain(tot_a.at[pl.ds(0, n - 1)], small_recv.at[3])
-    for k in range(n):
-        keep(first + k // 2, k % 2, tot_a[k])
-    ready.run(1, 2, stop, begin_0)
+    drain(land_a.at[pl.ds(0, n - 1)], small_recv.at[2])
+    tot_a[me] = jnp.sum(land_a[...], axis=0)
+    for peer in peers:
+        push(tot_a.at[me], tot_a.at[me], "fsdp", peer, small_send.at[3], small_recv.at[3])
+    for u in range(2, 2 * RAW):
+        push_0(u)
     sums.run(some, experts, experts, sums_z)
     spare = half * share - 2 * (experts - second)
     if spare:
@@ -225,7 +270,10 @@
     for peer, at in zip(near, near_at):
         push(part_z.at[at], land_z.at[mine], "fsdp", peer, small_send.at[4], small_recv.at[4])
     land_z[mine] = part_z[mine]
-    ready.run(2, 3, stop, begin_0)
+    drain(tot_a.at[pl.ds(0, n - 1)], small_recv.at[3])
+    for k in range(n):
+        keep(first + k // 2, k % 2, tot_a[k])
+    ready.run(first, first + 1, stop, begin_0)
     drain(land_z.at[pl.ds(0, half - 1)], small_recv.at[4])
     sum_z[...] = jnp.sum(land_z[...], axis=0)
     push(sum_z, far_z, "fsdp", far, small_send.at[5], small_recv.at[5])
@@ -233,12 +281,12 @@
     for peer in near:
         push(rows_r.at[me], rows_r.at[me], "fsdp", peer, r_send.at[1], r_recv.at[1])
         push(rows_r.at[far], rows_r.at[far], "fsdp", peer, r_send.at[1], r_recv.at[1])
-    ready.run(3, 4, stop, begin_0)
+    ready.run(first + 1, first + 2, stop, begin_0)
     drain(far_z, small_recv.at[5])
     tot_z[mine] = sum_z[...] + far_z[...]
     for peer in near:
         push(tot_z.at[mine], tot_z.at[mine], "fsdp", peer, small_send.at[6], small_recv.at[6])
-    ready.run(4, second, stop, begin_0)
+    ready.run(first + 2, second, stop, begin_0)
     drain(tot_z.at[pl.ds(0, half - 1)], small_recv.at[6])
 
     def keep_z(i, _):
@@ -250,6 +298,8 @@
     lax.fori_loop(0, experts - second, keep_z, 0)
     ready.run(second, cut, stop, begin_0)
     ready.run(cut, stop, stop, begin_1)
+    for u in range(2 * RAW):
+        end_0(u)
     drain(rows_r.at[pl.ds(0, n - 2)], r_recv.at[1])
     for twin in twins:
         push(rows_r, all_r.at[group], "ep", twin, r_send.at[2], r_recv.at[2])
@@ -260,8 +310,10 @@
         block = all_r[:, f].astype(f32)
         block = block.reshape(block.shape[0] * block.shape[1], depth)
         router[f * depth:(f + 1) * depth, :] = block.T.astype(bf16)
-    for m in range(2):
-        drain(land_0.at[m, pl.ds(0, n - 1)], small_send.at[m])
+    for u in range(2 * RAW):
+        drain(part_0.at[u, pl.ds(0, n - 1)], sum_send.at[u])
+        drain(send.at[0, 0, pl.ds(0, width - piece), :], raw_send.at[u])
+        drain(raw_land.at[u], raw_out.at[u])
     drain(part_a.at[pl.ds(0, n - 1)], small_send.at[2])
     drain(tot_a.at[pl.ds(0, n - 1)], small_send.at[3])
     drain(part_z.at[pl.ds(0, half - 1)], small_send.at[4])
@@ -271,7 +323,7 @@
     drain(rows_r.at[pl.ds(0, n - 2)], r_send.at[1])
     if p > 1:
         drain(all_r.at[pl.ds(0, p - 1)], r_send.at[2])
-    finish(n, cut, send, readys, own_sem.at[0], send_sem.at[0], recv_sem.at[0])
+    finish(n, cut - RAW, send, readys, own_sem.at[0], send_sem.at[0], recv_sem.at[0])
 
     @pl.when(odd)
     def _():
@@ -405,7 +457,7 @@
     piece = width // n
     columns = router_weight.shape[1]
     half = n // 2
-    share = -(-2 * (experts - 1 - half) // half)
+    share = -(-2 * (experts - RAW - half) // half)
     tail = experts // 32
     more = 3 * experts // 16
     cut = experts - tail - more
@@ -429,7 +481,9 @@
             pltpu.VMEM((2, SLOTS, depth, width), f32),
             pltpu.VMEM((2, SLOTS, depth, width), bf16),
             pltpu.VMEM((2, bulk, width, depth), bf16),
-            pltpu.VMEM((2, n, 1, width), f32),
+            pltpu.VMEM((2 * RAW, piece, n * depth), bf16),
+            *[pltpu.VMEM((2 * RAW, n, 1, 128), f32)] * 2,
+            pltpu.VMEM((1, width), f32),
             *[pltpu.VMEM((n, 1, width), f32)] * 3,
             *[pltpu.VMEM((half, share, width), f32)] * 2,
             *[pltpu.VMEM((share, width), f32)] * 2,
@@ -437,7 +491,7 @@
             pltpu.VMEM((n, columns, depth), bf16),
             pltpu.VMEM((p, n, columns, depth), bf16),
             dma((2, 2, SLOTS)), dma((2, 2, SLOTS)), dma((2, 2)), dma((2, 2)), dma((2, 2)),
-            dma((7,)), dma((7,)), dma((3,)), dma((3,)),
+            dma((7,)), dma((7,)), dma((3,)), dma((3,)), *[dma((2 * RAW,))] * 5,
         ],
         compiler_params=pltpu.CompilerParams(
             collective_id=0, has_side_effects=True, vmem_limit_bytes=60 * 2**20
@@ -493,7 +547,8 @@
         experts, depth, width = args[0].shape
         fits = (
             depth % 128 == 0 and width % (16 * n) == 0 and width % 128 == 0 and n % 4 == 0
-            and experts % 32 == 0 and experts >= n + 8 and args[4].shape[1] % 16 == 0
+            and experts % 32 == 0 and experts >= n + 8 and width <= 128 * n
+            and depth <= 256 and args[4].shape[1] % 16 == 0
             and 2 * experts * depth * width * 2 <= 2**25
         )
         return sending_device(n, p, *args) if fits else plain_device(*args)

time: 556 us -> 554 us (level)
  no operation moved by 1% of the time
where the time goes in v3:
time: 554 us; the launch traced here: 549 us
  Pallas kernels  547 us (99%)
    pallas_call x1, Pallas kernels, sending_device(): pl.pallas_call(functools.partial(bulk_kernel, n, p, cut, more), out_shape...  460 us
    pallas_call x1, Pallas kernels, sending_device(): pl.pallas_call(functools.partial(rest_kernel, n, cut, more), out_shape=(s...  69.3 us
    pallas_call x1, Pallas kernels, sending_device(): pl.pallas_call(functools.partial(place_kernel, n, cut, more), out_shape=(...  15.7 us

profile of v3, /device:TPU:0, one launch (start us, length us, event | category | flops | bytes accessed | tf_op | source)
XLA Modules:
  0.0 548.7 jit_solution(8419543785583255788)
XLA Ops:
  0.6 459.8 %send_bulk.1 = (bf16[31,96,2048]{2,1,0:T(8,128)(2,1)}, bf16[31,96,2048]{2,1,0:T(8,128)(2,1)}, f32[32,768]{1,0:T(8,128)}, f32[32,768]{1,0:T(8,128)}, bf16[2048,128]{1,0:T(8,128)(2,1)}) custom-call(f32[32,256,768]{2,1,0:T(8,128)} %tg.3, bf16[32,256,768]{2,1,0:T(8,128)(2,1)} %og.3, f32[32,256,768]{2,1,0:T(8,128)} %tu.3, bf16[32,256,768]{2,1,0:T(8,128)(2,1)} %ou.3, ...), custom_call_target="tpu_custom_call" | custom-call | tf_op jit(solution)/shard_map/send_bulk/pallas_call | solution.py:473
  460.4 0.0 copy-start
  460.5 0.0 copy-start.1
  460.5 15.7 %place_bulk.1 = (bf16[32,96,2048]{2,1,0:T(8,128)(2,1)}, bf16[32,96,2048]{2,1,0:T(8,128)(2,1)}, f32[32,96]{1,0:T(8,128)}, f32[32,96]{1,0:T(8,128)}, bf16[2048,128]{1,0:T(8,128)(2,1)}) custom-call(bf16[31,96,2048]{2,1,0:T(8,128)(2,1)} %get-tuple-element.21.got_gate, bf16[31,96,2048]{2,1,0:T(8,128)(2,1)} %get-tuple-element.22.got_up, ...), custom_call_target="tpu_custom_call" | custom-call | tf_op jit(solution)/shard_map/place_bulk/pallas_call | solution.py:501
  476.2 0.0 copy-done
  476.2 0.0 copy-done.1
  476.2 0.0 copy-start.2
  476.2 0.7 copy-done.2
  476.9 69.3 %send_rest.1 = (bf16[7,96,2048]{2,1,0:T(8,128)(2,1)S(1)}, bf16[7,96,2048]{2,1,0:T(8,128)(2,1)S(1)}) custom-call(f32[32,256,768]{2,1,0:T(8,128)} %tg.3, bf16[32,256,768]{2,1,0:T(8,128)(2,1)} %og.3, f32[32,256,768]{2,1,0:T(8,128)} %tu.3, bf16[32,256,768]{2,1,0:T(8,128)(2,1)} %ou.3, f32[32,768]{1,0:T(8,128)S(1)} %copy-done, f32[32,768]{1,0:T(8,128)S(1)} %copy-done.1, ...), custom_call_target="tpu_custom_call" | custom-call | tf_op jit(solution)/shard_map/send_rest/pallas_call | solution.py:514
  546.2 2.5 place_rest.1
Async XLA Ops:
  460.4 15.7 %copy-start = (f32[32,768]{1,0:T(8,128)S(1)}, f32[32,768]{1,0:T(8,128)}, u32[]{:S(2)}) copy-start(f32[32,768]{1,0:T(8,128)} %get-tuple-element.19.scale_gate) | copy-start | bytes 294916
  460.5 15.7 %copy-start.1 = (f32[32,768]{1,0:T(8,128)S(1)}, f32[32,768]{1,0:T(8,128)}, u32[]{:S(2)}) copy-start(f32[32,768]{1,0:T(8,128)} %get-tuple-element.20.scale_up) | copy-start | bytes 294916
  476.2 0.7 copy-start.2
